TPU v7x, 16 devices: a whole 2x2x2 slice. The times are simulated.
16 devices in a mesh: rows: 16 (over z, y, x, core).
Axes of the slice: x: 2, y: 2, z: 2, core: 2. Of those that a mesh axis runs over, the one named last changes fastest.
Arguments:
- a_mat: float32 [262144, 64], P('rows')
- b_mat: float32 [262144, 4], P('rows')
Outputs:
- output 1: float32 [262144, 64], P('rows')
- output 2: float32 [64, 64], replicated
- output 3: float32 [64, 4], replicated
All inputs are finite; a program needn't handle non-finite values.
Results may differ from a plain program's by a relative error of at most 0.001.
Values sent between devices are 32-bit elements.
A program may use at most 1 GiB of HBM per device.

v0:
```python
import jax
import jax.numpy as jnp
from jax import lax
from jax.experimental import pallas as pl
from jax.experimental.pallas import tpu as pltpu
from jax.sharding import PartitionSpec as P


HI = lax.Precision.HIGHEST
F32 = jnp.float32
N = 64
RHS = 4
BLK = 8
LANES = 128
CHIPS = 8
PIECES = (2048, 4096, 5120, 5120)
SUB = 1024
AHEAD = 3
STORES = (2048,) * 7 + (1024,) * 2
HALF = N // 2
MSG = HALF + BLK
FAR_FIRST = (7, 6, 5, 3, 4, 2, 1)
NT, NN, TN = ((1,), (1,)), ((1,), (0,)), ((0,), (0,))
MESH = pl.DeviceIdType.MESH


def _dot(x, y, dims, precision=None):
    return lax.dot_general(x, y, (dims, ((), ())), precision=precision, preferred_element_type=F32)


def _two_sum(a, b):
    s = a + b
    t = s - a
    return s, (a - (s - t)) + (b - t)


def _scale(x, axis):
    q = jnp.max(jnp.abs(x), axis=axis, keepdims=True) * 8388609.0
    return jnp.abs(q - q * (1.0 - 2.0 ** -24))


def _slices(x, p):
    s1, s2, s3 = p * (1.5 * 2.0 ** 16), p * (1.5 * 2.0 ** 8), p * 1.5
    h1 = (x + s1) - s1
    r1 = x - h1
    h2 = (r1 + s2) - s2
    r2 = r1 - h2
    h3 = (r2 + s3) - s3
    return h1, h2, h3, r2 - h3


def _split3(x):
    c = x * 65537.0
    h1 = c - (c - x)
    r = x - h1
    c = r * 65537.0
    h2 = c - (c - r)
    return h1, h2, r - h2


def _gram_chunk(x, b, px, acc):
    s1, e1, g2, g3, gc = acc
    for q in range(x.shape[1] // SUB):
        h1, h2, h3, l = _slices(x[:, q * SUB:(q + 1) * SUB], px)
        c1, c2, c3 = _split3(b[:, q * SUB:(q + 1) * SUB])
        o = _dot(jnp.concatenate([h1, h2, h3, l], axis=0), jnp.concatenate([h1, h2, c1, c2, c3], axis=0), NT)
        s1, err = _two_sum(s1, o[:N, :2 * N])
        e1 = e1 + err
        g2 = g2 + o[N:2 * N, :2 * N]
        g3 = g3 + (o[2 * N:3 * N, :2 * N] + o[3 * N:, :2 * N])
        gc = gc + ((o[:N, 2 * N:] + o[N:2 * N, 2 * N:]) + (o[2 * N:3 * N, 2 * N:] + o[3 * N:, 2 * N:]))
    return s1, e1, g2, g3, gc


def _gram_finish(acc):
    s1, e1, g2, g3, gc = acc
    cross = s1[:, N:]
    small = e1[:, N:] + (g3[:, :N] + g3[:, N:])
    z, ez = _two_sum(cross, cross.T)
    h, ea = _two_sum(s1[:, :N], z)
    h, eb = _two_sum(h, g2[:, N:])
    lo = ((ea + eb) + ez) + e1[:, :N] + (small + small.T)
    hi, lo = _two_sum(h, lo)
    ct = gc.T
    ct = ct[:RHS] + (ct[RHS:2 * RHS] + ct[2 * RHS:])
    return hi, lo, ct


def _pack(hi, lo, bta):
    both = jnp.concatenate([hi, lo], axis=1)
    row = lax.broadcasted_iota(jnp.int32, (HALF, LANES), 0)
    col = lax.broadcasted_iota(jnp.int32, (HALF, LANES), 1) % N
    block = jnp.where(col - HALF > row, jnp.roll(both[:HALF], HALF, axis=1), both[HALF:])
    diag = jnp.sum(jnp.where(row == col, both[:HALF], 0.0), axis=0, keepdims=True)
    sub = lax.broadcasted_iota(jnp.int32, (BLK, LANES), 0)
    tail = jnp.concatenate([jnp.zeros((RHS, LANES), F32), jnp.concatenate([bta, jnp.zeros_like(bta)], axis=1)], axis=0)
    return jnp.concatenate([block, jnp.where(sub == 0, diag, tail)], axis=0)


def _unpack(block, diag):
    row = lax.broadcasted_iota(jnp.int32, (HALF, HALF), 0)
    col = lax.broadcasted_iota(jnp.int32, (HALF, HALF), 1)
    cross, tri = block[:, :HALF], block[:, HALF:]
    flip = tri.T
    first = jnp.where(row == col, diag[:, :HALF], jnp.where(col > row, tri, flip))
    last = jnp.where(col <= row, tri, flip)
    return jnp.concatenate([jnp.concatenate([first, cross.T], axis=1), jnp.concatenate([cross, last], axis=1)], axis=0)


def _fold(both, err):
    lane = lax.broadcasted_iota(jnp.int32, both.shape, 1)
    sub = lax.broadcasted_iota(jnp.int32, both.shape, 0)
    return both + jnp.where((lane >= N) & (sub <= HALF), jnp.roll(err, N, axis=1), 0.0)


def _row(v, k):
    return jnp.broadcast_to(v[k:k + 1, :], (BLK, LANES))


def _factor(g):
    row = lax.broadcasted_iota(jnp.int32, (N, N), 0)
    col = lax.broadcasted_iota(jnp.int32, (N, N), 1)
    full = jnp.concatenate([g, jnp.where(row == col, 1.0, 0.0)], axis=1)
    blocks = N // BLK
    w = [full[BLK * i:BLK * i + BLK] for i in range(blocks)]
    sub = lax.broadcasted_iota(jnp.int32, (BLK, LANES), 0)
    spread = lambda blk, p: [jnp.broadcast_to(blk[:, BLK * p + j:BLK * p + j + 1], (BLK, LANES)) for j in range(BLK)]
    diag = spread(w[0], 0)
    pivot = _row(diag[0], 0)
    out = []
    for p in range(blocks):
        below = [spread(blk, p) for blk in w[p + 1:]]
        ahead = spread(w[p + 1], p + 1) if p + 1 < blocks else None
        cur, pivots_done = w[p], pivot
        for k in range(BLK):
            inv = 1.0 / pivot
            if k > 0:
                pivots_done = jnp.where(sub == k, pivot, pivots_done)
            if k + 1 < BLK:
                link, pivot = _row(diag[k], k + 1), _row(diag[k + 1], k + 1)
                pivot = pivot - (link * link) * inv
            elif ahead is not None:
                link, pivot = _row(below[0][k], 0), _row(ahead[0], 0)
                pivot = pivot - (link * link) * inv
            tops = [_row(diag[j], k) for j in range(k + 1, BLK)]
            mult = jnp.where(sub > k, diag[k], 0.0) * inv
            urow = _row(cur, k)
            for j in range(k + 1, BLK):
                diag[j] = diag[j] - mult * tops[j - k - 1]
            cur = cur - mult * urow
            for i, cols in enumerate(below):
                scaled = cols[k] * inv
                for j in range(k + 1, BLK):
                    cols[j] = cols[j] - scaled * tops[j - k - 1]
                w[p + 1 + i] = w[p + 1 + i] - scaled * urow
                if i == 0:
                    ahead = [ahead[j] - scaled * _row(cols[k], j) for j in range(BLK)]
        out.append(cur * lax.rsqrt(pivots_done))
        diag = ahead
    out = jnp.concatenate(out, axis=0)
    return jnp.where(col >= row, out[:, :N], 0.0), jnp.where(col <= row, out[:, N:], 0.0)


def _exact_rest(first, o1, o2, o3, o4):
    blk = lambda o, i: o[N * i:N * i + N]
    t, e = _two_sum(first, -blk(o1, 0))
    t, ea = _two_sum(t, -blk(o1, 1))
    t, eb = _two_sum(t, -blk(o2, 0))
    t, ec = _two_sum(t, -blk(o2, 1))
    rest = (blk(o1, 2) + blk(o3, 0)) + (blk(o1, 3) + blk(o4, 0)) + ((blk(o2, 2) + blk(o3, 1)) + (blk(o2, 3) + blk(o4, 1)))
    rest = rest + ((blk(o3, 2) + blk(o4, 3)) + (blk(o3, 3) + blk(o4, 2)))
    return (t - rest) + ((e + ea) + (eb + ec))


def _refined(hi, lo):
    row = lax.broadcasted_iota(jnp.int32, (N, N), 0)
    col = lax.broadcasted_iota(jnp.int32, (N, N), 1)
    eye = jnp.where(row == col, 1.0, 0.0)
    r1, v = _factor(jnp.where(row == col, hi * (1.0 + 2.0 ** -19), hi))
    parts = _slices(r1, _scale(r1, 0))
    left = jnp.concatenate(parts, axis=1)
    f = _exact_rest(hi, *[_dot(left, part, TN) for part in parts]) + lo
    left = jnp.concatenate(_slices(v, _scale(v, 1)), axis=0)
    d = _exact_rest(eye, *[_dot(left, part, NT) for part in _slices(r1, _scale(r1, 1))])
    d = jnp.where(col <= row, d, 0.0)
    e = _dot(_dot(v, f, NN, HI), v, NT, HI) + (_dot(d, d, NT, HI) - (d + d.T))
    r2, v2 = _factor(eye + e)
    return r2, r1 + _dot(d, r1, TN, HI), v2, v


def _reduce_kernel(a_hbm, b_hbm, f_ref, bta_ref, a_buf, b_buf, slots, sums, a_sem, b_sem, send_sem, recv_sem, down_sem):
    me = lax.axis_index('rows')
    core = me % 2
    chip = me // 2
    partner = me + 1 - 2 * core
    steps = len(PIECES)
    edges = [sum(PIECES[:i]) for i in range(steps + 1)]
    copies = []
    for i in range(steps):
        win = pl.ds(edges[i], PIECES[i])
        copies.append(pltpu.make_async_copy(a_hbm.at[:, win], a_buf.at[:, win], a_sem.at[i]))
    b_copy = pltpu.make_async_copy(b_hbm, b_buf, b_sem)
    for copy in copies[:1] + [b_copy] + copies[1:AHEAD]:
        copy.start()
    barrier = pltpu.get_barrier_semaphore()
    x, y, z = chip % 2, (chip // 2) % 2, chip // 4
    flip = lambda bit, way: 1 - bit if way else bit
    peers = [8 * flip(z, far // 4) + 4 * flip(y, far // 2 % 2) + 2 * flip(x, far % 2) + core for far in FAR_FIRST]
    for peer in peers + [partner]:
        pl.semaphore_signal(barrier, inc=1, device_id=(peer,), device_id_type=MESH)

    zero = jnp.zeros((N, 2 * N), F32)
    acc = (zero, zero, zero, zero, jnp.zeros((N, 3 * RHS), F32))
    scale = None
    for i in range(steps + 1):
        nxt = None
        if i < steps:
            copies[i].wait()
            if i + AHEAD < steps:
                copies[i + AHEAD].start()
            nxt = _scale(a_buf[:, edges[i]:edges[i + 1]], 1)
        if i == 0:
            b_copy.wait()
        if i > 0:
            win = slice(edges[i - 1], edges[i])
            acc = _gram_chunk(a_buf[:, win], b_buf[:, win], scale, acc)
        scale = nxt
    hi, lo, bta = _gram_finish(acc)
    slots[pl.ds(chip, 1)] = _pack(hi, lo, bta)[None]
    pl.semaphore_wait(barrier, CHIPS)
    sends = [pltpu.make_async_remote_copy(
        src_ref=slots.at[chip], dst_ref=slots.at[chip], send_sem=send_sem.at[j], recv_sem=recv_sem.at[j],
        device_id=(peer,), device_id_type=MESH) for j, peer in enumerate(peers)]
    for send in sends:
        send.start()
    for send in sends:
        send.wait_recv()
    both, err = slots[0], jnp.zeros((MSG, LANES), F32)
    for j in range(1, CHIPS):
        both, e = _two_sum(both, slots[j])
        err = err + e
    sums[pl.ds(core, 1)] = _fold(both, err)[None]
    swap = pltpu.make_async_remote_copy(
        src_ref=sums.at[core], dst_ref=sums.at[core], send_sem=down_sem.at[0], recv_sem=down_sem.at[1],
        device_id=(partner,), device_id_type=MESH)
    swap.start()
    swap.wait_recv()
    got = _fold(*_two_sum(sums[0], sums[1]))
    r2, rc, v2, v = _refined(*[_unpack(got[:HALF, side:side + N], got[HALF:HALF + 1, side:side + N]) for side in (0, N)])
    f_ref[:, :LANES] = jnp.concatenate([r2, rc], axis=1)
    f_ref[:, LANES:] = jnp.concatenate([v2, v], axis=1)
    bta_ref[...] = got[HALF:, :]
    for send in sends:
        send.wait_send()
    swap.wait_send()


def _apply_kernel(f_ref, bta_ref, a_ref, q_hbm, r_hbm, c_hbm, q_buf, r_buf, c_buf, q_sem, small_sem):
    inv_t = _dot(f_ref[:, LANES:LANES + N], f_ref[:, LANES + N:], NN, HI)
    w = jnp.concatenate([jnp.concatenate([m] * 3, axis=1) for m in _split3(inv_t)], axis=0)
    copies = []
    start = 0
    for i, size in enumerate(STORES):
        win = pl.ds(start, size)
        o = _dot(w, jnp.concatenate(_split3(a_ref[:, win]), axis=0), NN)
        q_buf[:, win] = o[:N] + (o[N:2 * N] + o[2 * N:])
        copies.append(pltpu.make_async_copy(q_buf.at[:, win], q_hbm.at[:, win], q_sem.at[i]))
        copies[-1].start()
        start += size
        if i == 0:
            row = lax.broadcasted_iota(jnp.int32, (N, N), 0)
            col = lax.broadcasted_iota(jnp.int32, (N, N), 1)
            r_buf[...] = jnp.where(col >= row, _dot(f_ref[:, :N], f_ref[:, N:LANES], NN, HI), 0.0)
            c_buf[...] = _dot(bta_ref[:, :N], inv_t, NT, HI)[RHS:]
            copies.append(pltpu.make_async_copy(r_buf, r_hbm, small_sem.at[0]))
            copies.append(pltpu.make_async_copy(c_buf, c_hbm, small_sem.at[1]))
            copies[-2].start()
            copies[-1].start()
    for copy in copies:
        copy.wait()


def solution(mesh):
    def local_fn(a_blk, b_blk):
        a_t, b_t = a_blk.T, b_blk.T
        rows = a_t.shape[1]
        factors, bta, a_vmem = pl.pallas_call(
            _reduce_kernel,
            out_shape=[pltpu.VMEM((N, 2 * LANES), F32), pltpu.VMEM((BLK, LANES), F32), pltpu.VMEM((N, rows), F32)],
            in_specs=[pl.BlockSpec(memory_space=pltpu.HBM)] * 2,
            out_specs=[pl.BlockSpec(memory_space=pltpu.VMEM)] * 3,
            scratch_shapes=[
                pltpu.VMEM((RHS, rows), F32),
                pltpu.VMEM((CHIPS, MSG, LANES), F32),
                pltpu.VMEM((2, MSG, LANES), F32),
                pltpu.SemaphoreType.DMA((len(PIECES),)),
                pltpu.SemaphoreType.DMA,
                pltpu.SemaphoreType.DMA((CHIPS - 1,)),
                pltpu.SemaphoreType.DMA((CHIPS - 1,)),
                pltpu.SemaphoreType.DMA((2,)),
            ],
            compiler_params=pltpu.CompilerParams(collective_id=0, has_side_effects=True, vmem_limit_bytes=62_700_000),
        )(a_t, b_t)
        q_t, r, c_t = pl.pallas_call(
            _apply_kernel,
            out_shape=[jax.ShapeDtypeStruct((N, rows), F32), jax.ShapeDtypeStruct((N, N), F32), jax.ShapeDtypeStruct((RHS, N), F32)],
            in_specs=[pl.BlockSpec(memory_space=pltpu.VMEM)] * 3,
            out_specs=[pl.BlockSpec(memory_space=pltpu.HBM)] * 3,
            scratch_shapes=[
                pltpu.VMEM((N, rows), F32),
                pltpu.VMEM((N, N), F32),
                pltpu.VMEM((RHS, N), F32),
                pltpu.SemaphoreType.DMA((len(STORES),)),
                pltpu.SemaphoreType.DMA((2,)),
            ],
            compiler_params=pltpu.CompilerParams(vmem_limit_bytes=48 * 2 ** 20),
        )(factors, bta, a_vmem)
        return q_t.T, r, c_t.T

    return jax.shard_map(local_fn, mesh=mesh, in_specs=(P('rows', None), P('rows', None)), out_specs=(P('rows', None), P(), P()), check_vma=False)
```

profile of v0, /device:TPU:1, one launch (start us, length us, event | category | flops | bytes accessed | tf_op | source)
XLA Modules:
  0.0 20.5 jit_solution(5102645896977036815)
XLA Ops:
  0.6 16.8 %shard_map.49 = (f32[64,256]{1,0:T(8,128)S(1)}, f32[8,128]{1,0:T(8,128)S(1)}, f32[64,16384]{1,0:T(8,128)S(1)}) custom-call(f32[64,16384]{1,0:T(8,128)} %bitcast.4, f32[4,16384]{1,0:T(4,128)} %bitcast.5), custom_call_target="tpu_custom_call" | custom-call | tf_op jit(solution)/shard_map/pallas_call | solution.py:287
  17.4 3.2 %shard_map.50 = (f32[64,16384]{1,0:T(8,128)}, f32[64,64]{1,0:T(8,128)}, f32[4,64]{1,0:T(4,128)}) custom-call(f32[64,256]{1,0:T(8,128)S(1)} %get-tuple-element.9.f_ref, f32[8,128]{1,0:T(8,128)S(1)} %get-tuple-element.10.bta_ref, f32[64,16384]{1,0:T(8,128)S(1)} %get-tuple-element.11.a_ref), custom_call_target="tpu_custom_call" | custom-call | tf_op jit(solution)/shard_map/pallas_call | solution.py:304
where the time goes:
time: 20.7 us; the launch traced here: 20.5 us
  Pallas kernels  19.9 us (96%)
  between operations  0.64 us (3%)
    pallas_call x1, Pallas kernels, local_fn(): pl.pallas_call(_reduce_kernel, out_shape=[pltpu.VMEM((N, 2 * LANES), F32)...  16.8 us
    pallas_call x1, Pallas kernels, local_fn(): pl.pallas_call(_apply_kernel, out_shape=[jax.ShapeDtypeStruct((N, rows),...  3.15 us

commit v1 on v0

--- a/solution.py
+++ b/solution.py
@@ -59,29 +59,30 @@
 
 
 def _gram_chunk(x, b, px, acc):
-    s1, e1, g2, g3, gc = acc
+    s1, e1, g2, g3, ga, gb = acc
     for q in range(x.shape[1] // SUB):
         h1, h2, h3, l = _slices(x[:, q * SUB:(q + 1) * SUB], px)
         c1, c2, c3 = _split3(b[:, q * SUB:(q + 1) * SUB])
-        o = _dot(jnp.concatenate([h1, h2, h3, l], axis=0), jnp.concatenate([h1, h2, c1, c2, c3], axis=0), NT)
+        o = _dot(jnp.concatenate([h1, h2, h3, l], axis=0), jnp.concatenate([h1, h2, h3 + l, c1, c2, c3], axis=0), NT)
         s1, err = _two_sum(s1, o[:N, :2 * N])
         e1 = e1 + err
         g2 = g2 + o[N:2 * N, :2 * N]
         g3 = g3 + (o[2 * N:3 * N, :2 * N] + o[3 * N:, :2 * N])
-        gc = gc + ((o[:N, 2 * N:] + o[N:2 * N, 2 * N:]) + (o[2 * N:3 * N, 2 * N:] + o[3 * N:, 2 * N:]))
-    return s1, e1, g2, g3, gc
+        ga = ga + (o[:N, 2 * N:] + o[N:2 * N, 2 * N:])
+        gb = gb + (o[2 * N:3 * N, 2 * N:] + o[3 * N:, 2 * N:])
+    return s1, e1, g2, g3, ga, gb
 
 
 def _gram_finish(acc):
-    s1, e1, g2, g3, gc = acc
+    s1, e1, g2, g3, ga, gb = acc
     cross = s1[:, N:]
     small = e1[:, N:] + (g3[:, :N] + g3[:, N:])
     z, ez = _two_sum(cross, cross.T)
     h, ea = _two_sum(s1[:, :N], z)
     h, eb = _two_sum(h, g2[:, N:])
-    lo = ((ea + eb) + ez) + e1[:, :N] + (small + small.T)
+    lo = ((ea + eb) + ez) + e1[:, :N] + (small + small.T) + gb[:, :N]
     hi, lo = _two_sum(h, lo)
-    ct = gc.T
+    ct = (ga + gb)[:, N:].T
     ct = ct[:RHS] + (ct[RHS:2 * RHS] + ct[2 * RHS:])
     return hi, lo, ct
 
@@ -210,7 +211,8 @@
         pl.semaphore_signal(barrier, inc=1, device_id=(peer,), device_id_type=MESH)
 
     zero = jnp.zeros((N, 2 * N), F32)
-    acc = (zero, zero, zero, zero, jnp.zeros((N, 3 * RHS), F32))
+    wide = jnp.zeros((N, N + 3 * RHS), F32)
+    acc = (zero, zero, zero, zero, wide, wide)
     scale = None
     for i in range(steps + 1):
         nxt = None

time: 20.7 us -> 22 us (1.063)
  Pallas kernels: 19.9 us -> 21.2 us
    pallas_call x1, Pallas kernels: 16.8 us -> 18.1 us  [local_fn(): pl.pallas_call(_reduce_kernel, out_shape=[pltpu.VMEM((N, 2 * LANES), F32)...]
where the time goes in v1:
time: 22 us; the launch traced here: 21.9 us
  Pallas kernels  21.2 us (96%)
  between operations  0.64 us (3%)
    pallas_call x1, Pallas kernels, local_fn(): pl.pallas_call(_reduce_kernel, out_shape=[pltpu.VMEM((N, 2 * LANES), F32)...  18.1 us
    pallas_call x1, Pallas kernels, local_fn(): pl.pallas_call(_apply_kernel, out_shape=[jax.ShapeDtypeStruct((N, rows),...  3.15 us

profile of v1, /device:TPU:1, one launch (start us, length us, event | category | flops | bytes accessed | tf_op | source)
XLA Modules:
  0.0 21.9 jit_solution(13468336450414429246)
XLA Ops:
  0.6 18.1 %shard_map.49 = (f32[64,256]{1,0:T(8,128)S(1)}, f32[8,128]{1,0:T(8,128)S(1)}, f32[64,16384]{1,0:T(8,128)S(1)}) custom-call(f32[64,16384]{1,0:T(8,128)} %bitcast.4, f32[4,16384]{1,0:T(4,128)} %bitcast.5), custom_call_target="tpu_custom_call" | custom-call | tf_op jit(solution)/shard_map/pallas_call | solution.py:289
  18.7 3.2 %shard_map.50 = (f32[64,16384]{1,0:T(8,128)}, f32[64,64]{1,0:T(8,128)}, f32[4,64]{1,0:T(4,128)}) custom-call(f32[64,256]{1,0:T(8,128)S(1)} %get-tuple-element.9.f_ref, f32[8,128]{1,0:T(8,128)S(1)} %get-tuple-element.10.bta_ref, f32[64,16384]{1,0:T(8,128)S(1)} %get-tuple-element.11.a_ref), custom_call_target="tpu_custom_call" | custom-call | tf_op jit(solution)/shard_map/pallas_call | solution.py:306
